TPU v7x, 256 devices: a whole 4x4x8 slice. The times are simulated.
256 devices in a mesh: slab: 128 (over x, z, y), pencil: 2 (over core).
Axes of the slice: x: 4, y: 4, z: 8, core: 2. Of those that a mesh axis runs over, the one named last changes fastest.
Arguments:
- density: float32 [768, 768, 384], P('slab', 'pencil'), may hold values from 0 to 1
- cell_kind: int32 [768, 768, 384], P('slab', 'pencil'), may hold values from 0 to 2
- sharpness: float32 [1], replicated, may hold values from 48 to 96
- fraction: float32 [1], replicated, may hold values from 0.36 to 0.41
Outputs:
- physical: float32 [768, 768, 384], P('slab', 'pencil')
- threshold: float32 [1], replicated
Inputs may be any that keep to these rules, and one draw needn't show every extreme that they name: `cell_kind`: each cell is a design, void or solid cell.
All inputs are finite; a program needn't handle non-finite values.
Results may differ from a plain program's by a relative error of at most 0.0003.
Values sent between devices are 32-bit elements; how exact they have to be, the bound alone decides.
A program may use at most 128 MiB of HBM per device.

v0:
```python
import functools

import jax
import jax.numpy as jnp
from jax import lax
from jax.sharding import Mesh
from jax.sharding import PartitionSpec as P

RADIUS = 5
ITERS = 3
SLAB = ("slab_0", "slab_1", "slab_2")


def extended(x, sides, width):
    for axis, dim in sides:
        size, length = (lax.axis_size(axis), x.shape[dim])
        up = [(i, (i + 1) % size) for i in range(size - 1)]
        down = [(j, i) for i, j in up]
        last = lax.slice_in_dim(x, length - width, length, axis=dim)
        leading = lax.slice_in_dim(x, 0, width, axis=dim)
        before = lax.ppermute(last, axis, up)
        after = lax.ppermute(leading, axis, down)
        x = jnp.concatenate([before, x, after], axis=dim)
    return x


def one_axis_at_a_time(x, axes):
    return functools.reduce(lax.psum, axes, x)


def filter_padded(padded, axis, length):
    total = None
    for offset in range(-RADIUS, RADIUS + 1):
        weight = float(RADIUS + 1 - abs(offset))
        piece = lax.slice_in_dim(padded, RADIUS + offset, RADIUS + offset + length, axis=axis)
        total = weight * piece if total is None else total + weight * piece
    return total


def coverage_local(count, start, whole):
    index = start + jnp.arange(count, dtype=jnp.int32)
    total = jnp.zeros((count,), jnp.float32)
    for offset in range(-RADIUS, RADIUS + 1):
        inside = ((index + offset >= 0) & (index + offset < whole)).astype(jnp.float32)
        total = total + float(RADIUS + 1 - abs(offset)) * inside
    return total


def project(filtered, cell_kind, beta, level):
    tangent = jnp.tanh(beta * (filtered - level))
    design = cell_kind == 0
    solid = cell_kind == 2
    values = jnp.where(design, 0.5 * (1.0 + tangent), jnp.where(solid, 1.0, 0.0))
    return (values, tangent, design)


def local(density, cell_kind, sharpness, fraction):
    depth, rows, cols = density.shape
    slabs = lax.axis_size(SLAB)
    pencils = lax.axis_size("pencil")
    padded = extended(density, ((SLAB, 0),), RADIUS)
    along_z = filter_padded(padded, 0, depth)
    widened = extended(along_z, (("pencil", 1),), RADIUS)
    along_y = filter_padded(widened, 1, rows)
    along_x = filter_padded(jnp.pad(along_y, ((0, 0), (0, 0), (RADIUS, RADIUS))), 2, cols)
    cover_z = coverage_local(depth, lax.axis_index(SLAB) * depth, depth * slabs)
    cover_y = coverage_local(rows, lax.axis_index("pencil") * rows, rows * pencils)
    cover_x = coverage_local(cols, jnp.int32(0), cols)
    cover = cover_z[:, None, None] * cover_y[None, :, None] * cover_x[None, None, :]
    filtered = along_x / cover
    beta = sharpness[0]
    cells = jnp.float32(depth * slabs * rows * pencils * cols)
    level = jnp.float32(0.5)
    for step in range(ITERS):
        values, tangent, design = project(filtered, cell_kind, beta, level)
        volume_part = jnp.sum(values)
        slope_part = jnp.sum(jnp.where(design, 0.5 * beta * (1.0 - tangent * tangent), 0.0))
        inner = lax.psum((volume_part, slope_part), "pencil")
        volume, slope_sum = (one_axis_at_a_time(inner[0], SLAB), one_axis_at_a_time(inner[1], SLAB))
        level = level + (volume - fraction[0] * cells) / (cells + slope_sum)
    values, tangent, design = project(filtered, cell_kind, beta, level)
    return (values, jnp.reshape(level, (1,)))


def solution(mesh):
    split = Mesh(
        mesh.devices.reshape(4, 8, 4, mesh.shape["pencil"]),
        ("slab_0", "slab_1", "slab_2", "pencil"),
    )
    return jax.shard_map(
        local,
        mesh=split,
        in_specs=(P(SLAB, "pencil", None), P(SLAB, "pencil", None), P(), P()),
        out_specs=(P(SLAB, "pencil", None), P()),
        check_vma=False,
    )
```

profile of v0, /device:TPU:2, one launch (start us, length us, event | category | flops | bytes accessed | tf_op | source)
XLA Modules:
  0.0 261.6 jit_solution(13821397172465933471)
XLA Ops:
  0.6 4.8 %fusion.142 = (f32[5,384,384]{2,1,0:T(8,128)S(1)}, f32[5,384,384]{2,1,0:T(8,128)}) fusion(f32[6,384,384]{2,1,0:T(8,128)} %param.4), kind=kLoop, calls=%fused_computation.216 | loop fusion | bytes 11796480 | tf_op jit(solution)/shard_map/slice | solution.py:19
  5.4 3.5 %collective-permute-start = (f32[5,384,384]{2,1,0:T(8,128)S(1)}, f32[5,384,384]{2,1,0:T(8,128)}, u32[]{:S(2)}, u32[]{:S(2)}) collective-permute-start(f32[5,384,384]{2,1,0:T(8,128)S(1)} %get-tuple-element.39), channel_id=1, source_target_pairs={{0,2},{2,4},{4,6},{6,8},{8,10},{10,12},{12,14},{14,16},{16,18},{18... | collective-permute-start | bytes 8847368 | tf_op jit(solution)/shard_map/ppermute | solution.py:21
  8.9 8.6 %collective-permute-start.1 = (f32[5,384,384]{2,1,0:T(8,128)}, f32[5,384,384]{2,1,0:T(8,128)}, u32[]{:S(2)}, u32[]{:S(2)}) collective-permute-start(f32[5,384,384]{2,1,0:T(8,128)} %get-tuple-element.40), channel_id=1, source_target_pairs={{2,0},{4,2},{6,4},{8,6},{10,8},{12,10},{14,12},{16,14},{18,16},{20... | collective-permute-start | bytes 8847368 | tf_op jit(solution)/shard_map/ppermute | solution.py:22
  17.6 0.1 broadcast_multiply_fusion
  17.7 61.9 %collective-permute-done = f32[5,384,384]{2,1,0:T(8,128)} collective-permute-done((f32[5,384,384]{2,1,0:T(8,128)S(1)}, f32[5,384,384]{2,1,0:T(8,128)}, u32[]{:S(2)}, u32[]{:S(2)}) %collective-permute-start) | collective-permute-done | bytes 2949152 | tf_op jit(solution)/shard_map/ppermute | solution.py:21
  79.6 2.0 constant_dynamic-update-slice_fusion.1
  81.6 2.6 constant_dynamic-update-slice_fusion
  84.2 0.0 collective-permute-done.1
  84.3 2.0 constant_dynamic-update-slice_fusion.2
  86.3 5.0 %slice_add_fusion = f32[6,384,384]{2,1,0:T(8,128)} fusion(f32[11,384,384]{2,1,0:T(8,128)S(1)} %constant_dynamic-update-slice_fusion.2, f32[11,384,384]{2,1,0:T(8,128)S(1)} %get-tuple-element.37, f32[6,384,384]{2,1,0:T(8,128)} %param.4), kind=kLoop, calls=%fused_computation.76 | loop fusion | flops 16809984 | bytes 42467328 | tf_op jit(solution)/shard_map/add | solution.py:36
  91.3 0.9 fusion.141
  92.2 1.3 collective-permute-start.2
  93.5 1.3 collective-permute-start.3
  96.1 0.0 copy-start
  96.1 0.0 collective-permute-done.2
  96.1 0.5 collective-permute-done.3
  96.7 21.1 %fusion.25 = f32[6,384,384]{2,1,0:T(8,128)S(1)} fusion(f32[6,5,384]{2,1,0:T(8,128)S(1)} %collective-permute-done.3, f32[6,5,384]{2,1,0:T(8,128)S(1)} %collective-permute-done.2, f32[6,384,384]{2,1,0:T(8,128)} %slice_add_fusion), kind=kLoop, calls=%fused_computation.47 | loop fusion | flops 25657344 | bytes 7170048 | tf_op jit(solution)/shard_map/add | solution.py:36
  117.8 0.0 copy-done
  117.8 11.4 %select_reduce_fusion.2 = (f32[]{:T(128)}, f32[]{:T(128)}, f32[6,384,384]{2,1,0:T(8,128)S(1)}, pred[6,384,384]{2,1,0:T(8,128)(4,1)}, pred[6,384,384]{2,1,0:T(8,128)(4,1)}) fusion(f32[]{:T(128)S(6)} %mul.340, f32[]{:T(128)} %bitcast.7, f32[384]{0:T(512)S(1)} %convert_add_fusion, f32[6,384]{1,0:T(8,128)S(1)} %broadcast_multiply_fusion, ...), kind=kLoop, calls=%fused_computation.98 | loop fusion | flops 30965760 | bytes 12397072 | tf_op jit(solution)/shard_map/reduce_sum | solution.py:77
  129.2 3.4 %all-reduce.12 = (f32[]{:T(128)}, f32[]{:T(128)}) all-reduce(f32[]{:T(128)} %get-tuple-element.7, f32[]{:T(128)} %get-tuple-element.6), channel_id=1, replica_groups=mesh['slab_0'=4,'slab_1'=8,'slab_2'=4,'pencil'=2] {'pencil'}, use_global_device_ids=true, to_apply=%region_1.2 | all-reduce | flops 2 | bytes 16 | tf_op jit(solution)/shard_map/psum | solution.py:78
  132.6 9.2 %all-reduce.9 = (f32[]{:T(128)}, f32[]{:T(128)}) all-reduce(f32[]{:T(128)} %get-tuple-element.30, f32[]{:T(128)} %get-tuple-element.31), channel_id=1, replica_groups=mesh['slab_0'=4,'slab_1'=8,'slab_2'=4,'pencil'=2] {'slab_0'}, use_global_device_ids=true, to_apply=%region_2.3 | all-reduce | flops 2 | bytes 16 | tf_op jit(solution)/shard_map/psum | solution.py:28
  141.8 16.2 %all-reduce.3 = (f32[]{:T(128)}, f32[]{:T(128)}) all-reduce(f32[]{:T(128)} %get-tuple-element.24, f32[]{:T(128)} %get-tuple-element.25), channel_id=1, replica_groups=mesh['slab_0'=4,'slab_1'=8,'slab_2'=4,'pencil'=2] {'slab_1'}, use_global_device_ids=true, to_apply=%region_3.4 | all-reduce | flops 2 | bytes 16 | tf_op jit(solution)/shard_map/psum | solution.py:28
  158.0 10.9 %all-reduce.6 = (f32[]{:T(128)}, f32[]{:T(128)}) all-reduce(f32[]{:T(128)} %get-tuple-element.12, f32[]{:T(128)} %get-tuple-element.13), channel_id=1, replica_groups=mesh['slab_0'=4,'slab_1'=8,'slab_2'=4,'pencil'=2] {'slab_2'}, use_global_device_ids=true, to_apply=%region_4.5 | all-reduce | flops 2 | bytes 16 | tf_op jit(solution)/shard_map/psum | solution.py:28
  170.3 4.0 %select_reduce_fusion.1 = (f32[]{:T(128)}, f32[]{:T(128)}) fusion(pred[6,384,384]{2,1,0:T(8,128)(4,1)} %get-tuple-element.34, f32[6,384,384]{2,1,0:T(8,128)S(1)} %get-tuple-element.32, f32[]{:T(128)S(6)} %add.745, f32[]{:T(128)S(6)} %mul.340, f32[]{:T(128)} %bitcast.6, pred[6,384,384]{2,1,0:T(8,128)(4,1)} %get-tuple-element.33), kind=kLoop, calls=%fused_computation.96 | loop fusion | flops 10616830 | bytes 5308436 | tf_op jit(solution)/shard_map/reduce_sum | solution.py:77
  174.2 3.1 %all-reduce.11 = (f32[]{:T(128)}, f32[]{:T(128)}) all-reduce(f32[]{:T(128)} %get-tuple-element.5, f32[]{:T(128)} %get-tuple-element.4), channel_id=1, replica_groups=mesh['slab_0'=4,'slab_1'=8,'slab_2'=4,'pencil'=2] {'pencil'}, use_global_device_ids=true, to_apply=%region_11.12 | all-reduce | flops 2 | bytes 16 | tf_op jit(solution)/shard_map/psum | solution.py:78
  177.3 9.5 %all-reduce.8 = (f32[]{:T(128)}, f32[]{:T(128)}) all-reduce(f32[]{:T(128)} %get-tuple-element.28, f32[]{:T(128)} %get-tuple-element.29), channel_id=1, replica_groups=mesh['slab_0'=4,'slab_1'=8,'slab_2'=4,'pencil'=2] {'slab_0'}, use_global_device_ids=true, to_apply=%region_12.13 | all-reduce | flops 2 | bytes 16 | tf_op jit(solution)/shard_map/psum | solution.py:28
  186.8 14.8 %all-reduce.2 = (f32[]{:T(128)}, f32[]{:T(128)}) all-reduce(f32[]{:T(128)} %get-tuple-element.22, f32[]{:T(128)} %get-tuple-element.23), channel_id=1, replica_groups=mesh['slab_0'=4,'slab_1'=8,'slab_2'=4,'pencil'=2] {'slab_1'}, use_global_device_ids=true, to_apply=%region_13.14 | all-reduce | flops 2 | bytes 16 | tf_op jit(solution)/shard_map/psum | solution.py:28
  201.6 10.0 %all-reduce.5 = (f32[]{:T(128)}, f32[]{:T(128)}) all-reduce(f32[]{:T(128)} %get-tuple-element.10, f32[]{:T(128)} %get-tuple-element.11), channel_id=1, replica_groups=mesh['slab_0'=4,'slab_1'=8,'slab_2'=4,'pencil'=2] {'slab_2'}, use_global_device_ids=true, to_apply=%region_14.15 | all-reduce | flops 2 | bytes 16 | tf_op jit(solution)/shard_map/psum | solution.py:28
  212.9 4.0 %select_reduce_fusion = (f32[]{:T(128)}, f32[]{:T(128)}) fusion(pred[6,384,384]{2,1,0:T(8,128)(4,1)} %get-tuple-element.34, f32[6,384,384]{2,1,0:T(8,128)S(1)} %get-tuple-element.32, f32[]{:T(128)S(6)} %add.748, f32[]{:T(128)S(6)} %mul.340, f32[]{:T(128)} %bitcast.5, pred[6,384,384]{2,1,0:T(8,128)(4,1)} %get-tuple-element.33), kind=kLoop, calls=%fused_computation.94 | loop fusion | flops 10616830 | bytes 5308436 | tf_op jit(solution)/shard_map/reduce_sum | solution.py:77
  216.9 3.1 %all-reduce.10 = (f32[]{:T(128)}, f32[]{:T(128)}) all-reduce(f32[]{:T(128)} %get-tuple-element.3, f32[]{:T(128)} %get-tuple-element.2), channel_id=1, replica_groups=mesh['slab_0'=4,'slab_1'=8,'slab_2'=4,'pencil'=2] {'pencil'}, use_global_device_ids=true, to_apply=%region_21.22 | all-reduce | flops 2 | bytes 16 | tf_op jit(solution)/shard_map/psum | solution.py:78
  220.0 8.3 %all-reduce.7 = (f32[]{:T(128)}, f32[]{:T(128)}) all-reduce(f32[]{:T(128)} %get-tuple-element.26, f32[]{:T(128)} %get-tuple-element.27), channel_id=1, replica_groups=mesh['slab_0'=4,'slab_1'=8,'slab_2'=4,'pencil'=2] {'slab_0'}, use_global_device_ids=true, to_apply=%region_22.23 | all-reduce | flops 2 | bytes 16 | tf_op jit(solution)/shard_map/psum | solution.py:28
  228.4 16.0 %all-reduce.1 = (f32[]{:T(128)}, f32[]{:T(128)}) all-reduce(f32[]{:T(128)} %get-tuple-element.20, f32[]{:T(128)} %get-tuple-element.21), channel_id=1, replica_groups=mesh['slab_0'=4,'slab_1'=8,'slab_2'=4,'pencil'=2] {'slab_1'}, use_global_device_ids=true, to_apply=%region_23.24 | all-reduce | flops 2 | bytes 16 | tf_op jit(solution)/shard_map/psum | solution.py:28
  244.3 10.4 %all-reduce.4 = (f32[]{:T(128)}, f32[]{:T(128)}) all-reduce(f32[]{:T(128)} %get-tuple-element.8, f32[]{:T(128)} %get-tuple-element.9), channel_id=1, replica_groups=mesh['slab_0'=4,'slab_1'=8,'slab_2'=4,'pencil'=2] {'slab_2'}, use_global_device_ids=true, to_apply=%region_24.25 | all-reduce | flops 2 | bytes 16 | tf_op jit(solution)/shard_map/psum | solution.py:28
  256.0 4.5 %select_select_fusion = f32[6,384,384]{2,1,0:T(8,128)} fusion(pred[6,384,384]{2,1,0:T(8,128)(4,1)} %get-tuple-element.34, pred[6,384,384]{2,1,0:T(8,128)(4,1)} %get-tuple-element.33, f32[6,384,384]{2,1,0:T(8,128)S(1)} %get-tuple-element.32, f32[]{:T(128)} %add.751, f32[]{:T(128)} %bitcast.3), kind=kLoop, calls=%fused_computation.18 | loop fusion | flops 5308416 | bytes 8847368 | tf_op jit(solution)/shard_map/jit(_where)/select_n | solution.py:53
  (3 shorter events, 0.1 us)
Async XLA Ops:
  5.4 74.2 %collective-permute-start = (f32[5,384,384]{2,1,0:T(8,128)S(1)}, f32[5,384,384]{2,1,0:T(8,128)}, u32[]{:S(2)}, u32[]{:S(2)}) collective-permute-start(f32[5,384,384]{2,1,0:T(8,128)S(1)} %get-tuple-element.39), channel_id=1, source_target_pairs={{0,2},{2,4},{4,6},{6,8},{8,10},{10,12},{12,14},{14,16},{16,18},{18... | collective-permute-start | bytes 8847368 | tf_op jit(solution)/shard_map/ppermute | solution.py:21
  8.9 75.4 %collective-permute-start.1 = (f32[5,384,384]{2,1,0:T(8,128)}, f32[5,384,384]{2,1,0:T(8,128)}, u32[]{:S(2)}, u32[]{:S(2)}) collective-permute-start(f32[5,384,384]{2,1,0:T(8,128)} %get-tuple-element.40), channel_id=1, source_target_pairs={{2,0},{4,2},{6,4},{8,6},{10,8},{12,10},{14,12},{16,14},{18,16},{20... | collective-permute-start | bytes 8847368 | tf_op jit(solution)/shard_map/ppermute | solution.py:22
  92.2 3.9 %collective-permute-start.2 = (f32[6,5,384]{2,1,0:T(8,128)S(1)}, f32[6,5,384]{2,1,0:T(8,128)S(1)}, u32[]{:S(2)}, u32[]{:S(2)}) collective-permute-start(f32[6,5,384]{2,1,0:T(8,128)S(1)} %get-tuple-element.35), channel_id=1, source_target_pairs={{0,1},{2,3},{4,5},{6,7},{8,9},{10,11},{12,13},{14,15},{16,17},{18,... | collective-permute-start | bytes 138248 | tf_op jit(solution)/shard_map/ppermute | solution.py:21
  93.5 3.2 %collective-permute-start.3 = (f32[6,5,384]{2,1,0:T(8,128)S(1)}, f32[6,5,384]{2,1,0:T(8,128)S(1)}, u32[]{:S(2)}, u32[]{:S(2)}) collective-permute-start(f32[6,5,384]{2,1,0:T(8,128)S(1)} %get-tuple-element.36), channel_id=1, source_target_pairs={{1,0},{3,2},{5,4},{7,6},{9,8},{11,10},{13,12},{15,14},{17,16},{19,... | collective-permute-start | bytes 138248 | tf_op jit(solution)/shard_map/ppermute | solution.py:22
  96.1 21.6 %copy-start = (s32[6,384,384]{2,1,0:T(8,128)S(1)}, s32[6,384,384]{2,1,0:T(8,128)}, u32[]{:S(2)}) copy-start(s32[6,384,384]{2,1,0:T(8,128)} %param.5) | copy-start | bytes 10616836
where the time goes:
time: 262 us
  blocking collectives  115 us (44%)
  waiting for transfers between devices  62.4 us (24%)
  other arithmetic  50 us (19%)
  starting transfers between devices  14.7 us (6%)
  local copies, waits for them, and re-layouts  12.4 us (5%)
  between operations  7.22 us (3%)
    psum x9, blocking collectives, one_axis_at_a_time(): return functools.reduce(lax.psum, axes, x)  105 us
    ppermute x2, waiting for transfers between devices, extended(): before = lax.ppermute(last, axis, up)  61.9 us
    add x2, other arithmetic, filter_padded(): total = weight * piece if total is None else total + weight * piece  26 us
    reduce_sum x3, other arithmetic, local(): jnp.sum(jnp.where(design, 0.5 * beta * (1.0 - tangent * tangent), 0.0))  19.4 us
    ppermute x2, starting transfers between devices, extended(): after = lax.ppermute(leading, axis, down)  9.92 us
    psum x3, blocking collectives, local(): inner = lax.psum((volume_part, slope_part), 'pencil')  9.56 us
    slice x2, local copies, waits for them, and re-layouts, extended(): last = lax.slice_in_dim(x, length - width, length, axis=dim)  5.72 us
  transfers between devices with their start and end apart: 4, of which 2 were waited for; matrix products, arithmetic and copies ran while one was open for 2% of the time, Pallas kernels for 0%

commit v1 on v0

v1 whole, which is shorter than its diff:
```python
import functools

import jax
import jax.numpy as jnp
from jax import lax
from jax.experimental import pallas as pl
from jax.experimental.pallas import tpu as pltpu
from jax.sharding import PartitionSpec as P

RADIUS = 5
ITERS = 3
LANES = 128
MESH = pl.DeviceIdType.MESH
FAR = 1e30

CHUNK = 24

NXC, NZC, NYC = 4, 8, 4


def torus_distance(d, n):
    return min(d, n - d)


PLANE = sorted(
    [(dx, dy) for dx in range(NXC) for dy in range(NYC) if (dx, dy) != (0, 0)],
    key=lambda o: -(torus_distance(o[0], NXC) + torus_distance(o[1], NYC)),
)
COLUMN = sorted(
    [(dz, dc) for dz in range(NZC) for dc in range(2) if (dz, dc) != (0, 0)],
    key=lambda o: -torus_distance(o[0], NZC),
)


def coverage_of(index, whole):
    low = jnp.maximum(float(RADIUS) - index, 0.0)
    high = jnp.maximum(index - float(whole - 1 - RADIUS), 0.0)
    full = float((RADIUS + 1) ** 2)
    return full - 0.5 * low * (low + 1.0) - 0.5 * high * (high + 1.0)


def two_boxes(x, axis):
    n = x.shape[axis]
    two = x + pltpu.roll(x, n - 1, axis)
    four = two + pltpu.roll(two, n - 2, axis)
    six = four + pltpu.roll(two, n - 4, axis)
    two = six + pltpu.roll(six, 1, axis)
    four = two + pltpu.roll(two, 2, axis)
    return four + pltpu.roll(two, 4, axis)


def filter_layers(v):
    before, own, after = v[:5], v[5:11], v[11:]
    suffix = [None] * 5
    suffix[4] = before[4]
    for m in range(3, -1, -1):
        suffix[m] = suffix[m + 1] + before[m]
    part_before = [None] * 6
    part_before[4] = suffix[4]
    for k in range(3, -1, -1):
        part_before[k] = part_before[k + 1] + suffix[k]
    prefix = [after[0]]
    for m in range(1, 5):
        prefix.append(prefix[-1] + after[m])
    part_after = [None] * 6
    part_after[1] = prefix[0]
    for k in range(2, 6):
        part_after[k] = part_after[k - 1] + prefix[k - 1]
    sums = [own[0]]
    for j in range(1, 6):
        sums.append(sums[-1] + own[j])
    total = sums[5]
    centre = [functools.reduce(jnp.add, sums)]
    for k in range(5):
        centre.append(centre[-1] + (total - 2.0 * sums[k]))
    out = []
    for k in range(6):
        value = centre[k]
        if part_before[k] is not None:
            value = value + part_before[k]
        if part_after[k] is not None:
            value = value + part_after[k]
        out.append(value)
    return out


def kernel(
    slabs,
    cells,
    density,
    cell_kind,
    sharpness,
    fraction,
    h_out,
    level_out,
    v,
    zf,
    kind,
    acc,
    part,
    recv_a,
    recv_b,
    send_low,
    send_high,
    recv_low,
    recv_high,
    own_sem,
    kind_sem,
    edge_sem,
    send_a,
    send_b,
    arrive_a,
    arrive_b,
):
    depth, rows, cols = density.shape
    steps = rows // CHUNK
    s = lax.axis_index("slab")
    c = lax.axis_index("pencil")
    cx = s // (NZC * NYC)
    cz = (s // NYC) % NZC
    cy = s % NYC

    def plane_peer(dx, dy):
        return {"slab": (((cx + dx) % NXC) * NZC + cz) * NYC + (cy + dy) % NYC, "pencil": c}

    def column_peer(dz, dc):
        return {"slab": (cx * NZC + (cz + dz) % NZC) * NYC + cy, "pencil": (c + dc) % 2}

    up, down = {"slab": s + 1, "pencil": c}, {"slab": s - 1, "pencil": c}
    has_up, has_down = s < slabs - 1, s > 0

    own_copy = pltpu.make_async_copy(density, v.at[5:11], own_sem)
    kind_copy = pltpu.make_async_copy(cell_kind, kind, kind_sem)
    own_copy.start()
    kind_copy.start()

    barrier = pltpu.get_barrier_semaphore()

    @pl.when(has_up)
    def _():
        pl.semaphore_signal(barrier, inc=1, device_id=up, device_id_type=MESH)

    @pl.when(has_down)
    def _():
        pl.semaphore_signal(barrier, inc=1, device_id=down, device_id_type=MESH)

    for offset in COLUMN:
        pl.semaphore_signal(barrier, inc=1, device_id=column_peer(*offset), device_id_type=MESH)
    for offset in PLANE:
        pl.semaphore_signal(barrier, inc=1, device_id=plane_peer(*offset), device_id_type=MESH)

    pl.semaphore_wait(barrier, len(COLUMN) + len(PLANE) + jnp.minimum(s, 1) + jnp.minimum(slabs - 1 - s, 1))

    def first_row(step):
        return pl.multiple_of(jnp.where(c == 1, step, steps - 1 - step) * CHUNK, 8)

    def upward(step):
        part_rows = pl.ds(first_row(step), CHUNK)
        return pltpu.make_async_remote_copy(
            src_ref=density.at[1:6, part_rows, :],
            dst_ref=v.at[0:5, part_rows, :],
            send_sem=send_low,
            recv_sem=recv_low.at[step],
            device_id=up,
            device_id_type=MESH,
        )

    def downward(step):
        part_rows = pl.ds(first_row(step), CHUNK)
        return pltpu.make_async_remote_copy(
            src_ref=density.at[0:5, part_rows, :],
            dst_ref=v.at[11:16, part_rows, :],
            send_sem=send_high,
            recv_sem=recv_high.at[step],
            device_id=down,
            device_id_type=MESH,
        )

    def send(step, carry):
        @pl.when(has_up)
        def _():
            upward(step).start()

        @pl.when(has_down)
        def _():
            downward(step).start()

        return carry

    lax.fori_loop(0, steps, send, 0)

    @pl.when(jnp.logical_not(has_down))
    def _():
        v[0:5] = jnp.zeros((5, rows, cols), jnp.float32)

    @pl.when(jnp.logical_not(has_up))
    def _():
        v[11:16] = jnp.zeros((5, rows, cols), jnp.float32)

    outer = pl.multiple_of(jnp.where(c == 0, 0, rows + 8), 8)
    zf[:, pl.ds(outer, 8), :] = jnp.zeros((depth, 8, cols), jnp.float32)
    acc[...] = jnp.zeros_like(acc)

    beta = sharpness[0]
    lane = lax.broadcasted_iota(jnp.int32, (1, cols), 1).astype(jnp.float32)
    over_x = 1.0 / coverage_of(lane, cols)

    edge_from = pl.multiple_of(jnp.where(c == 0, rows, 8), 8)
    edge = pltpu.make_async_remote_copy(
        src_ref=zf.at[:, pl.ds(edge_from, 8), :],
        dst_ref=zf.at[:, pl.ds(pl.multiple_of(jnp.where(c == 0, 0, rows + 8), 8), 8), :],
        send_sem=edge_sem.at[0],
        recv_sem=edge_sem.at[1],
        device_id={"slab": s, "pencil": 1 - c},
        device_id_type=MESH,
    )

    def along_z(step):
        start = first_row(step)
        for group in range(CHUNK // 8):
            at = pl.ds(pl.multiple_of(start + group * 8, 8), 8)
            to = pl.ds(pl.multiple_of(start + group * 8 + 8, 8), 8)
            for tile in range(cols // LANES):
                lanes = slice(tile * LANES, (tile + 1) * LANES)
                filtered = filter_layers([v[m, at, lanes] for m in range(16)])
                for k in range(depth):
                    zf[k, to, lanes] = filtered[k]

    def along_y_x(step):
        start = first_row(step)
        row = (c * rows + start + lax.broadcasted_iota(jnp.int32, (CHUNK, 1), 0)).astype(jnp.float32)
        scale = (beta / coverage_of(row, 2 * rows)) * over_x

        def layer(k, carry):
            block = zf[k, pl.ds(start, CHUNK + 16), :]
            y = two_boxes(block, 0)[8 : 8 + CHUNK]
            wide = jnp.concatenate([y, jnp.zeros((CHUNK, LANES), jnp.float32)], axis=1)
            x = two_boxes(wide, 1)[:, :cols]
            over_z = 1.0 / coverage_of(jnp.full((1, 1), s * depth + k, jnp.int32).astype(jnp.float32), depth * slabs)
            h = x * (scale * over_z)
            which = kind[k, pl.ds(start, CHUNK), :]
            h = jnp.where(which == 0, h, jnp.where(which == 2, FAR, -FAR))
            h_out[k, pl.ds(start, CHUNK), :] = h
            t = jnp.tanh(h - 0.5 * beta)
            q = 1.0 - t * t
            for group in range(CHUNK // 8):
                piece = slice(group * 8, group * 8 + 8)
                acc[0] += t[piece]
                acc[1] += q[piece]
            return carry

        lax.fori_loop(0, depth, layer, 0)

    own_copy.wait()

    def walk(step, carry):
        @pl.when(step == 1)
        def _():
            edge.start()

        @pl.when(has_down)
        def _():
            upward(step).wait_recv()

        @pl.when(has_up)
        def _():
            downward(step).wait_recv()

        along_z(step)

        @pl.when(step == 1)
        def _():
            edge.wait()
            kind_copy.wait()

        @pl.when(step >= 1)
        def _():
            along_y_x(step - 1)

        return carry

    lax.fori_loop(0, steps, walk, 0)
    along_y_x(steps - 1)

    def fold(x):
        total = x[:, :LANES]
        for tile in range(1, cols // LANES):
            total = total + x[:, tile * LANES : (tile + 1) * LANES]
        return jnp.sum(total, axis=0, keepdims=True)

    peers_a = [plane_peer(*offset) for offset in PLANE]
    peers_b = [column_peer(*offset) for offset in COLUMN]
    lane_index = lax.broadcasted_iota(jnp.int32, (1, LANES), 1)

    def copy_a(it, j):
        return pltpu.make_async_remote_copy(
            src_ref=part.at[it, 0],
            dst_ref=recv_a.at[it, j],
            send_sem=send_a.at[it],
            recv_sem=arrive_a.at[it],
            device_id=peers_a[j],
            device_id_type=MESH,
        )

    def copy_b(it, j):
        return pltpu.make_async_remote_copy(
            src_ref=part.at[it, 1],
            dst_ref=recv_b.at[it, j],
            send_sem=send_b.at[it],
            recv_sem=arrive_b.at[it],
            device_id=peers_b[j],
            device_id_type=MESH,
        )

    def everywhere(it, sums_t, sums_q):
        mine = jnp.where(
            lane_index == 0,
            jnp.sum(sums_t, axis=1, keepdims=True),
            jnp.where(lane_index == 1, jnp.sum(sums_q, axis=1, keepdims=True), 0.0),
        )
        part[it, 0] = mine
        for j in range(len(PLANE)):
            copy_a(it, j).start()
        pltpu.make_async_copy(recv_a.at[it], recv_a.at[it], arrive_a.at[it]).wait()
        for j in range(len(PLANE)):
            mine = mine + recv_a[it, j]
        part[it, 1] = mine
        for j in range(len(COLUMN)):
            copy_b(it, j).start()
        pltpu.make_async_copy(recv_b.at[it], recv_b.at[it], arrive_b.at[it]).wait()
        for j in range(len(COLUMN)):
            mine = mine + recv_b[it, j]
        return (
            jnp.sum(jnp.where(lane_index == 0, mine, 0.0), axis=1, keepdims=True),
            jnp.sum(jnp.where(lane_index == 1, mine, 0.0), axis=1, keepdims=True),
        )

    def next_level(it, level, sums_t, sums_q):
        sum_t, sum_q = everywhere(it, sums_t, sums_q)
        volume = 0.5 * (cells + sum_t)
        slope = cells + (0.5 * beta) * sum_q
        return level + (volume - fraction[0] * cells) / slope

    def sums_at(level):
        shift = jnp.broadcast_to(beta * level, (8, cols))

        def rows_of(r, carry):
            sum_t, sum_q = carry
            at = pl.ds(pl.multiple_of(r * 8, 8), 8)
            for k in range(depth):
                t = jnp.tanh(h_out[k, at, :] - shift)
                sum_t = sum_t + t
                sum_q = sum_q + (1.0 - t * t)
            return (sum_t, sum_q)

        zero = jnp.zeros((8, cols), jnp.float32)
        sum_t, sum_q = lax.fori_loop(0, rows // 8, rows_of, (zero, zero))
        return (fold(sum_t), fold(sum_q))

    level = next_level(0, jnp.full((1, 1), 0.5, jnp.float32), fold(acc[0]), fold(acc[1]))

    def newton(it, level):
        return next_level(it, level, *sums_at(level))

    level = lax.fori_loop(1, ITERS, newton, level)
    level_out[...] = jnp.broadcast_to(level, (8, LANES))

    @pl.when(has_up)
    def _():
        pltpu.make_async_copy(density.at[1:6], v.at[0:5], send_low).wait()

    @pl.when(has_down)
    def _():
        pltpu.make_async_copy(density.at[0:5], v.at[11:16], send_high).wait()

    for it in range(ITERS):
        pltpu.make_async_copy(recv_a.at[it], recv_a.at[it], send_a.at[it]).wait()
        pltpu.make_async_copy(recv_b.at[it], recv_b.at[it], send_b.at[it]).wait()


def local(slabs, pencils, density, cell_kind, sharpness, fraction):
    depth, rows, cols = density.shape
    steps = rows // CHUNK
    cells = float(depth * slabs * rows * pencils * cols)
    na, nb = len(PLANE), len(COLUMN)
    h, level = pl.pallas_call(
        functools.partial(kernel, slabs, cells),
        out_shape=(
            jax.ShapeDtypeStruct((depth, rows, cols), jnp.float32),
            jax.ShapeDtypeStruct((8, LANES), jnp.float32),
        ),
        in_specs=[
            pl.BlockSpec(memory_space=pl.ANY),
            pl.BlockSpec(memory_space=pl.ANY),
            pl.BlockSpec(memory_space=pltpu.SMEM),
            pl.BlockSpec(memory_space=pltpu.SMEM),
        ],
        out_specs=(
            pl.BlockSpec(memory_space=pltpu.VMEM),
            pl.BlockSpec(memory_space=pltpu.VMEM),
        ),
        scratch_shapes=[
            pltpu.VMEM((16, rows, cols), jnp.float32),
            pltpu.VMEM((depth, rows + 16, cols), jnp.float32),
            pltpu.VMEM((depth, rows, cols), jnp.int32),
            pltpu.VMEM((2, 8, cols), jnp.float32),
            pltpu.VMEM((ITERS, 2, 1, LANES), jnp.float32),
            pltpu.VMEM((ITERS, na, 1, LANES), jnp.float32),
            pltpu.VMEM((ITERS, nb, 1, LANES), jnp.float32),
            pltpu.SemaphoreType.DMA,
            pltpu.SemaphoreType.DMA,
            pltpu.SemaphoreType.DMA((steps,)),
            pltpu.SemaphoreType.DMA((steps,)),
            pltpu.SemaphoreType.DMA,
            pltpu.SemaphoreType.DMA,
            pltpu.SemaphoreType.DMA((2,)),
            pltpu.SemaphoreType.DMA((ITERS,)),
            pltpu.SemaphoreType.DMA((ITERS,)),
            pltpu.SemaphoreType.DMA((ITERS,)),
            pltpu.SemaphoreType.DMA((ITERS,)),
        ],
        compiler_params=pltpu.CompilerParams(
            collective_id=0, has_side_effects=True, vmem_limit_bytes=48 * 1024 * 1024
        ),
        name="filter_and_newton",
    )(density, cell_kind, sharpness, fraction)
    level = level[0, :1]
    values = 0.5 * (1.0 + jnp.tanh(h - sharpness[0] * level[0]))
    return (values, level)


def solution(mesh):
    return jax.shard_map(
        functools.partial(local, mesh.shape["slab"], mesh.shape["pencil"]),
        mesh=mesh,
        in_specs=(P("slab", "pencil", None), P("slab", "pencil", None), P(), P()),
        out_specs=(P("slab", "pencil", None), P()),
        check_vma=False,
    )
```

time: 262 us -> 118 us (0.45)
  the two profiles are of different devices: /device:TPU:2 before, /device:TPU:1 now
where the time goes in v1:
time: 118 us
  Pallas kernels  112 us (95%)
  between operations  2.58 us (2%)
  other arithmetic  2.26 us (2%)
    pallas_call x1, Pallas kernels, local(): pl.pallas_call(functools.partial(kernel, slabs, cells), out_shape=(jax.Sh...  112 us

profile of v1, /device:TPU:1, one launch (start us, length us, event | category | flops | bytes accessed | tf_op | source)
XLA Modules:
  0.0 117.7 jit_solution(4181844641851558587)
XLA Ops:
  1.9 112.4 %filter_and_newton.1 = (f32[6,384,384]{2,1,0:T(8,128)S(1)}, f32[8,128]{1,0:T(8,128)S(1)}) custom-call(f32[6,384,384]{2,1,0:T(8,128)} %density.1, s32[6,384,384]{2,1,0:T(8,128)} %cell_kind.1, f32[1]{0:T(128)} %copy.6.sharpness, f32[1]{0:T(128)S(6)} %copy.7.fraction), custom_call_target="tpu_custom_call" | custom-call | tf_op jit(solution)/shard_map/filter_and_newton/pallas_call | solution.py:386
  114.3 0.5 slice.3
  115.5 2.3 %add_multiply_fusion = f32[6,384,384]{2,1,0:T(8,128)} fusion(f32[6,384,384]{2,1,0:T(8,128)S(1)} %get-tuple-element.4, f32[]{:T(128)S(6)} %mul.9), kind=kLoop, calls=%fused_computation | loop fusion | flops 2654208 | bytes 7077892 | tf_op jit(solution)/shard_map/mul | solution.py:428
